TPU v7x, 256 devices: a whole 4x4x8 slice. The times are simulated.
256 devices in a mesh: seq: 32 (over y, z), batch: 8 (over x, core).
Axes of the slice: x: 4, y: 4, z: 8, core: 2. Of those that a mesh axis runs over, the one named last changes fastest.
Arguments:
- conv_input: bfloat16 [32768, 8192], P(('batch', 'seq')), parts along dimension 0, may hold values from -6 to 6
- gate_input: bfloat16 [32768, 8192], P(('batch', 'seq')), parts along dimension 0, may hold values from -6 to 6
- conv_weight: bfloat16 [4, 8192], P(None, 'seq'), may hold values from -3 to 3
- conv_bias: bfloat16 [8192], P('seq'), may hold values from -3 to 3
- x_weight: bfloat16 [8192, 288], P('seq'), may hold values from -0.0625 to 0.0625
- dt_gain: float32 [256], replicated, may hold values from 0.5 to 1.5
- dt_weight: bfloat16 [256, 8192], P(None, 'seq'), may hold values from -0.375 to 0.375
- dt_bias: float32 [8192], P('seq'), may hold values from -6.9 to -2.3
- a_log: float32 [16, 8192], P(None, 'seq'), may hold values from 0 to 2.77
- skip: float32 [8192], P('seq'), may hold values from 0.5 to 1.5
Outputs:
- mixed: bfloat16 [32768, 8192], P(('batch', 'seq')), parts along dimension 0
There are 8 independent parts, one for each index of `batch`. A program takes and returns all parts, laid end to end along the dimension named above; an argument that names none is the same for every part. Nothing has to cross between parts.
All inputs are finite; a program needn't handle non-finite values.
Results may differ from a plain program's by a relative error of at most 0.0085.
Values may be sent and summed in bfloat16 or wider, within the bound.
A program may use at most 128 MiB of HBM per device.

v0:
```python
import jax
import jax.numpy as jnp
from jax import lax
from jax.sharding import PartitionSpec as P


def passed_along(value, axis, steps):
    count = lax.axis_size(axis)
    initial, last = (max(0, -steps), min(count, count - steps))
    return lax.ppermute(value, axis, [(source, source + steps) for source in range(initial, last)])


def from_everyone(x, axis):
    copies = jnp.broadcast_to(x, (lax.axis_size(axis), *x.shape))
    return lax.all_to_all(copies, axis, split_axis=0, concat_axis=0, tiled=True)


def joined_along(parts, dim):
    parts = jnp.moveaxis(parts, 0, dim)
    dims = parts.shape
    return parts.reshape(*dims[:dim], dims[dim] * dims[dim + 1], *dims[dim + 2 :])


def gather_directly(x, axis, dim):
    parts = from_everyone(x, axis)
    return joined_along(parts, dim)


def causal_conv(prefix, inputs, weight, bias):
    rows = inputs.shape[0]
    width = weight.shape[0]
    padded = jnp.concatenate([prefix, inputs.astype(jnp.float32)], 0)
    total = bias.astype(jnp.float32)[None, :]
    for tap in range(width):
        total = total + weight[tap].astype(jnp.float32)[None, :] * padded[tap : tap + rows]
    return jax.nn.silu(total).astype(jnp.bfloat16)


def link_blocks(earlier, later):
    return (earlier[0] * later[0], later[0] * earlier[1] + later[1])


def selective_scan(step, xfloat, bmat, cmat, rate):
    span = 16
    length, chans = step.shape
    states = rate.shape[0]
    blocks = length // span
    step_rows = step.reshape(blocks, span * chans)
    drive_rows = (step * xfloat).reshape(blocks, span * chans)
    b_rows = bmat.reshape(blocks, span * states)
    c_rows = cmat.reshape(blocks, span * states)
    state = jnp.zeros((blocks, states, chans), jnp.float32)
    running = jnp.zeros((blocks, chans), jnp.float32)
    local_parts = []
    elapsed = []
    for place in range(span):
        step_now = step_rows[:, place * chans : (place + 1) * chans]
        drive_now = drive_rows[:, place * chans : (place + 1) * chans]
        b_now = b_rows[:, place * states : (place + 1) * states]
        c_now = c_rows[:, place * states : (place + 1) * states]
        state = (
            jnp.exp(step_now[:, None, :] * rate[None]) * state
            + b_now[:, :, None] * drive_now[:, None, :]
        )
        local_parts.append(jnp.sum(c_now[:, :, None] * state, axis=1))
        running = running + step_now
        elapsed.append(running)
    totals = jnp.exp(running[:, None, :] * rate[None])
    _, through = lax.associative_scan(link_blocks, (totals, state), axis=0)
    starts = jnp.concatenate([jnp.zeros((1, states, chans), jnp.float32), through[: blocks - 1]], 0)
    pieces = []
    for place in range(span):
        c_now = c_rows[:, place * states : (place + 1) * states]
        carried = jnp.sum(
            c_now[:, :, None] * jnp.exp(elapsed[place][:, None, :] * rate[None]) * starts, axis=1
        )
        pieces.append(local_parts[place] + carried)
    return jnp.concatenate(pieces, 1).reshape(length, chans)


def local(
    conv_input,
    gate_input,
    conv_weight,
    conv_bias,
    x_weight,
    dt_gain,
    dt_weight,
    dt_bias,
    a_log,
    skip,
):
    width = conv_weight.shape[0]
    rank = dt_weight.shape[0]
    states = a_log.shape[0]
    prior = passed_along(conv_input[conv_input.shape[0] - (width - 1) :], "seq", 1)
    params = gather_directly(jnp.concatenate([conv_weight, conv_bias[None, :]], 0), "seq", 1)
    outgoing = causal_conv(prior.astype(jnp.float32), conv_input, params[:width], params[width])
    local_proj = jnp.dot(
        outgoing,
        lax.all_gather(x_weight, "seq", axis=0, tiled=True),
        preferred_element_type=jnp.float32,
    )
    arrived, gate_part = (
        lax.all_to_all(outgoing, "seq", split_axis=1, concat_axis=0, tiled=True),
        lax.all_to_all(gate_input, "seq", split_axis=1, concat_axis=0, tiled=True),
    )
    proj = lax.all_gather(local_proj, "seq", axis=0, tiled=True)
    dt_low = proj[:, :rank]
    bmat = proj[:, rank : rank + states]
    cmat = proj[:, rank + states :]
    normed = (
        dt_low
        * lax.rsqrt(jnp.mean(dt_low * dt_low, axis=1, keepdims=True) + 1e-06)
        * dt_gain[None, :]
    ).astype(jnp.bfloat16)
    step = jax.nn.softplus(
        jnp.dot(normed, dt_weight, preferred_element_type=jnp.float32) + dt_bias[None, :]
    )
    rate = -jnp.exp(a_log)
    xfloat = arrived.astype(jnp.float32)
    scanned = selective_scan(step, xfloat, bmat, cmat, rate)
    y_out = (scanned + skip[None, :] * xfloat).astype(jnp.bfloat16)
    held = lax.optimization_barrier(y_out)
    gated = (held.astype(jnp.float32) * jax.nn.silu(gate_part.astype(jnp.float32))).astype(
        jnp.bfloat16
    )
    return lax.all_to_all(gated, "seq", split_axis=0, concat_axis=1, tiled=True)


def solution(mesh):
    return jax.shard_map(
        local,
        mesh=mesh,
        in_specs=(
            P(("batch", "seq"), None),
            P(("batch", "seq"), None),
            P(None, "seq"),
            P("seq"),
            P("seq", None),
            P(),
            P(None, "seq"),
            P("seq"),
            P(None, "seq"),
            P("seq"),
        ),
        out_specs=P(("batch", "seq"), None),
        check_vma=False,
    )
```

profile of v0, /device:TPU:32, one launch (start us, length us, event | category | flops | bytes accessed | tf_op | source)
XLA Modules:
  0.0 660.3 jit_solution(11097169348318939079)
XLA Ops:
  9.3 11.4 %all-to-all-start = ((bf16[32,5,256]{2,1,0:T(8,128)(2,1)}), bf16[32,5,256]{2,1,0:T(8,128)(2,1)S(1)}, u32[]{:S(2)}, u32[]{:S(2)}) async-start(bf16[32,5,256]{2,1,0:T(8,128)(2,1)} %broadcast_in_dim.7), calls=%async_computation | async-start | bytes 262144 | tf_op jit(solution)/shard_map/all_to_all | solution.py:15
  30.5 7.6 %multiply_convert_fusion.1 = bf16[128,8192]{1,0:T(8,128)(2,1)S(1)} fusion(f32[128,8192]{1,0:T(8,128)} %convert_element_type.94, f32[3,8192]{1,0:T(4,128)S(1)} %convert_element_type.93, f32[8192]{0:T(1024)S(1)} %bitcast.55, f32[8192]{0:T(1024)S(1)} %bitcast.56, f32[8192]{0:T(1024)S(1)} %bitcast.57, f32[8192]{0:T(1024)S(1)} %bitcast.58, f32[8192]{0:T(1024)S(1)} %bitcast.54), kind=kLoop, calls=%fused_computation.78 | loop fusion | flops 16777216 | bytes 6553600 | tf_op jit(solution)/shard_map/convert_element_type | solution.py:36
  38.2 59.4 %all-gather.3.cloned.1.call-done = bf16[8192,288]{0,1:T(8,128)(2,1)} async-done(((bf16[256,288]{0,1:T(8,128)(2,1)}), bf16[8192,288]{0,1:T(8,128)(2,1)}) %all-gather.3.cloned.1.call-update) | async-done | bytes 4718608 | tf_op jit(solution)/shard_map/all_gather | solution.py:101
  103.5 9.4 %all-to-all-start.1 = ((bf16[128,32,256]{2,0,1:T(8,128)(2,1)}), bf16[128,32,256]{2,0,1:T(8,128)(2,1)S(1)}, u32[]{:S(2)}, u32[]{:S(2)}) async-start(bf16[128,32,256]{2,0,1:T(8,128)(2,1)} %bitcast.50), calls=%async_computation.1 | async-start | bytes 4194304 | tf_op jit(solution)/shard_map/all_to_all | solution.py:105
  116.2 88.2 %all-gather.5.cloned.1.call-done = f32[4096,288]{0,1:T(8,128)} async-done(((f32[128,288]{0,1:T(8,128)}), f32[4096,288]{0,1:T(8,128)}) %all-gather.5.cloned.1.call-update) | async-done | bytes 4718608 | tf_op jit(solution)/shard_map/all_gather | solution.py:108
  206.9 9.4 %all-to-all-start.2 = ((bf16[128,32,256]{2,0,1:T(8,128)(2,1)}), bf16[128,32,256]{2,0,1:T(8,128)(2,1)}, u32[]{:S(2)}, u32[]{:S(2)}) async-start(bf16[128,32,256]{2,0,1:T(8,128)(2,1)} %bitcast.49), calls=%async_computation.2 | async-start | bytes 4194304 | tf_op jit(solution)/shard_map/all_to_all | solution.py:106
  216.4 8.7 %bitcast_multiply_fusion.2 = (f32[4096,256]{1,0:T(8,128)}, f32[4096,256]{1,0:T(8,128)}) fusion(bf16[128,32,256]{2,0,1:T(8,128)(2,1)S(1)} %all-to-all-done.1, f32[256]{0:T(256)S(1)} %copy-done.131, bf16[256,256]{1,0:T(8,128)(2,1)S(1)} %copy-done, f32[4096,288]{0,1:T(8,128)} %all-gather.5.cloned.1.call-done, f32[256]{0:T(256)S(1)} %copy-done.132, ...), kind=kOutput, calls=%fused_computation.23 | convolution fusion | flops 549453824 | bytes 14829568 | tf_op jit(solution)/shard_map/dot_general | solution.py:118
  254.2 20.0 %multiply_reduce_fusion.1 = (f32[256,256]{1,0:T(8,128)}, f32[256,16,256]{2,1,0:T(8,128)S(1)}, f32[256,16,256]{2,1,0:T(8,128)S(1)}, f32[256,16,256]{2,1,0:T(8,128)}) fusion(f32[256,16]{1,0:T(8,128)S(1)} %get-tuple-element.99, f32[256,256]{1,0:T(8,128)} %get-tuple-element.77, f32[256,16]{1,0:T(8,128)} %get-tuple-element.117, ...), kind=kLoop, calls=%fused_computation.27 | loop fusion | flops 69140480 | bytes 21528576 | tf_op jit(solution)/shard_map/reduce_sum | solution.py:65
  274.2 6.4 multiply_reduce_fusion.3
  323.2 8.7 %pad.59 = f32[32,16,256]{2,1,0:T(8,128)} pad(f32[16,16,256]{2,1,0:T(8,128)} %add.351, f32[]{:T(128)} %constant.5.clone.1), padding=1_0_1x0_0_0x0_0_0 | pad | bytes 786436 | tf_op jit(solution)/shard_map/pad | solution.py:69
  336.3 11.6 %pad.61 = f32[64,16,256]{2,1,0:T(8,128)S(1)} pad(f32[32,16,256]{2,1,0:T(8,128)} %add.353, f32[]{:T(128)} %constant.5.clone.1), padding=1_0_1x0_0_0x0_0_0 | pad | bytes 1572868 | tf_op jit(solution)/shard_map/pad | solution.py:69
  349.8 15.6 %pad.60 = f32[64,16,256]{2,1,0:T(8,128)} pad(f32[32,16,256]{2,1,0:T(8,128)} %pad_maximum_fusion.3, f32[]{:T(128)} %constant.5.clone.1), padding=0_1_1x0_0_0x0_0_0 | pad | bytes 1572868 | tf_op jit(solution)/shard_map/pad | solution.py:69
  369.8 23.1 %pad.62 = f32[128,16,256]{2,1,0:T(8,128)S(1)} pad(f32[64,16,256]{2,1,0:T(8,128)} %pad_maximum_fusion.2, f32[]{:T(128)} %constant.5.clone.1), padding=0_1_1x0_0_0x0_0_0 | pad | bytes 3145732 | tf_op jit(solution)/shard_map/pad | solution.py:69
  392.9 20.5 %pad.63 = f32[128,16,256]{2,1,0:T(8,128)} pad(f32[64,16,256]{2,1,0:T(8,128)S(1)} %copy-done.14, f32[]{:T(128)} %constant.5.clone.1), padding=1_0_1x0_0_0x0_0_0 | pad | bytes 3145732 | tf_op jit(solution)/shard_map/pad | solution.py:69
  422.5 9.2 %multiply_reduce_fusion.17 = f32[256,256]{1,0:T(8,128)} fusion(f32[256,16]{1,0:T(8,128)S(1)} %copy-done.103, f32[256,256]{1,0:T(8,128)S(1)} %copy-done.93, f32[256,16]{1,0:T(8,128)S(1)} %copy-done.128, f32[256,256]{1,0:T(8,128)S(1)} %copy-done.102, f32[16,256]{1,0:T(8,128)S(1)} %exponential_negate_fusion, f32[256,256]{1,0:T(8,128)S(1)} %copy-done.92, ...), kind=kLoop, calls=%fused_computation.43 | loop fusion | flops 35586048 | bytes 4620288 | tf_op jit(solution)/shard_map/reduce_sum | solution.py:65
  431.7 40.5 %pad.161 = f32[256,16,256]{2,1,0:T(8,128)} pad(f32[128,16,256]{2,1,0:T(8,128)S(1)} %copy-done.11, f32[]{:T(128)} %constant.5.clone.1), padding=1_0_1x0_0_0x0_0_0 | pad | bytes 6291460
  473.9 40.5 %pad.87 = f32[255,16,256]{2,1,0:T(8,128)} pad(f32[128,16,256]{2,1,0:T(8,128)S(1)} %pad_maximum_fusion.1, f32[]{:T(128)} %constant.5.clone.1), padding=0_0_1x0_0_0x0_0_0 | pad | bytes 6275076 | tf_op jit(solution)/shard_map/slice | solution.py:70
  514.5 8.7 %multiply_reduce_fusion.19 = f32[256,256]{1,0:T(8,128)S(1)} fusion(f32[256,16]{1,0:T(8,128)S(1)} %copy-done.105, f32[256,256]{1,0:T(8,128)} %get-tuple-element.86, f32[256,16]{1,0:T(8,128)} %get-tuple-element.126, f32[256,256]{1,0:T(8,128)} %get-tuple-element.87, f32[256,16]{1,0:T(8,128)} %get-tuple-element.127, f32[256,256]{1,0:T(8,128)} %get-tuple-element.65, ...), kind=kLoop, calls=%fused_computation.45 | loop fusion | flops 31391744 | bytes 4079616 | tf_op jit(solution)/shard_map/reduce_sum | solution.py:65
  531.2 9.1 %multiply_reduce_fusion.29 = (f32[256,256]{1,0:T(8,128)S(1)}, f32[256,256]{1,0:T(8,128)S(1)}, f32[256,256]{1,0:T(8,128)S(1)}, f32[256,256]{1,0:T(8,128)S(1)}, f32[256,256]{1,0:T(8,128)S(1)}, /*index=5*/f32[256,256]{1,0:T(8,128)S(1)}) fusion(f32[256,16]{1,0:T(8,128)S(1)} %copy-done.113, f32[256,256]{1,0:T(8,128)S(1)} %copy-done.87, ...), kind=kLoop, calls=%fused_computation.55 | loop fusion | flops 27918336 | bytes 7716864 | tf_op jit(solution)/shard_map/reduce_sum | solution.py:65
  541.1 7.6 %multiply_reduce_fusion.23 = (f32[256,256]{1,0:T(8,128)S(1)}, f32[256,256]{1,0:T(8,128)S(1)}, f32[256,256]{1,0:T(8,128)S(1)}) fusion(f32[256,16]{1,0:T(8,128)S(1)} %copy-done.110, f32[256,256]{1,0:T(8,128)S(1)} %copy-done.81, f32[256,16]{1,0:T(8,128)S(1)} %copy-done.117, f32[256,256]{1,0:T(8,128)S(1)} %copy-done.84, f32[256,16]{1,0:T(8,128)S(1)} %copy-done.119, ...), kind=kLoop, calls=%fused_computation.49 | loop fusion | flops 27066368 | bytes 3555328 | tf_op jit(solution)/shard_map/reduce_sum | solution.py:65
  548.9 8.8 %multiply_reduce_fusion = (f32[256,256]{1,0:T(8,128)S(1)}, f32[256,256]{1,0:T(8,128)S(1)}, f32[256,256]{1,0:T(8,128)S(1)}, f32[256,256]{1,0:T(8,128)S(1)}, f32[256,256]{1,0:T(8,128)S(1)}, /*index=5*/f32[256,256]{1,0:T(8,128)S(1)}) fusion(f32[256,16]{1,0:T(8,128)S(1)} %copy-done.108, f32[16,256]{1,0:T(8,128)S(1)} %exponential_negate_fusion, ...), kind=kLoop, calls=%fused_computation.26 | loop fusion | flops 24772608 | bytes 7438336 | tf_op jit(solution)/shard_map/reduce_sum | solution.py:74
  561.7 8.8 %multiply_reduce_fusion.2 = (f32[256,256]{1,0:T(8,128)S(1)}, f32[256,256]{1,0:T(8,128)S(1)}, f32[256,256]{1,0:T(8,128)S(1)}, f32[256,256]{1,0:T(8,128)S(1)}, f32[256,256]{1,0:T(8,128)S(1)}, /*index=5*/f32[256,256]{1,0:T(8,128)S(1)}) fusion(f32[256,256]{1,0:T(8,128)S(1)} %copy-done.57, f32[256,16]{1,0:T(8,128)S(1)} %copy-done.50, ...), kind=kLoop, calls=%fused_computation.28 | loop fusion | flops 24772608 | bytes 7438336 | tf_op jit(solution)/shard_map/reduce_sum | solution.py:74
  572.1 7.2 %multiply_reduce_fusion.9 = (f32[256,256]{1,0:T(8,128)S(1)}, f32[256,256]{1,0:T(8,128)S(1)}, f32[256,256]{1,0:T(8,128)S(1)}, f32[256,256]{1,0:T(8,128)S(1)}) fusion(f32[256,16]{1,0:T(8,128)S(1)} %copy-done.46, f32[256,256]{1,0:T(8,128)S(1)} %copy-done.27, f32[256,16]{1,0:T(8,128)S(1)} %copy-done.40, f32[256,256]{1,0:T(8,128)S(1)} %copy-done.37, ...), kind=kLoop, calls=%fused_computation.35 | loop fusion | flops 20709376 | bytes 6946816 | tf_op jit(solution)/shard_map/reduce_sum | solution.py:65
  596.8 55.1 %all_to_all.50 = bf16[32,128,256]{2,1,0:T(8,128)(2,1)S(1)} all-to-all(bf16[32,128,256]{2,1,0:T(8,128)(2,1)S(1)} %bitcast.48), channel_id=1, replica_groups=mesh['seq'=32,'batch'=8] {'seq'}, dimensions={0} | all-to-all | bytes 4194304 | tf_op jit(solution)/shard_map/all_to_all | solution.py:128
  (364 shorter events, 149.8 us)
Async XLA Ops:
  6.5 209.8 %copy-start = (bf16[256,256]{1,0:T(8,128)(2,1)S(1)}, bf16[256,256]{1,0:T(8,128)(2,1)}, u32[]{:S(2)}) copy-start(bf16[256,256]{1,0:T(8,128)(2,1)} %param.16) | copy-start | bytes 393220
  6.5 91.0 %all-gather.3.cloned.1.call-start = ((), (), s32[]{:S(2)}) async-start(), calls=%async_computation.4 | async-start | bytes 4866048 | tf_op jit(solution)/shard_map/all_gather | solution.py:101
  9.3 21.2 %all-to-all-start = ((bf16[32,5,256]{2,1,0:T(8,128)(2,1)}), bf16[32,5,256]{2,1,0:T(8,128)(2,1)S(1)}, u32[]{:S(2)}, u32[]{:S(2)}) async-start(bf16[32,5,256]{2,1,0:T(8,128)(2,1)} %broadcast_in_dim.7), calls=%async_computation | async-start | bytes 262144 | tf_op jit(solution)/shard_map/all_to_all | solution.py:15
  20.6 183.7 %all-gather.5.cloned.1.call-start = ((), (), s32[]{:S(2)}) async-start(), calls=%async_computation.5 | async-start | bytes 4866048 | tf_op jit(solution)/shard_map/all_gather | solution.py:108
  21.6 7.5 %collective-permute-start = (bf16[3,8192]{1,0:T(4,128)(2,1)S(1)}, bf16[3,8192]{1,0:T(4,128)(2,1)S(1)}, u32[]{:S(2)}, u32[]{:S(2)}) collective-permute-start(bf16[3,8192]{1,0:T(4,128)(2,1)S(1)} %slice.443), channel_id=1, source_target_pairs={{0,8},{8,16},{16,24},{24,32},{32,40},{40,48},{48,56},{56,64},{64,7... | collective-permute-start | bytes 147464 | tf_op jit(solution)/shard_map/ppermute | solution.py:10
  103.5 103.4 %all-to-all-start.1 = ((bf16[128,32,256]{2,0,1:T(8,128)(2,1)}), bf16[128,32,256]{2,0,1:T(8,128)(2,1)S(1)}, u32[]{:S(2)}, u32[]{:S(2)}) async-start(bf16[128,32,256]{2,0,1:T(8,128)(2,1)} %bitcast.50), calls=%async_computation.1 | async-start | bytes 4194304 | tf_op jit(solution)/shard_map/all_to_all | solution.py:105
  116.2 100.2 %copy-start.131 = (f32[256]{0:T(256)S(1)}, f32[256]{0:T(256)}, u32[]{:S(2)}) copy-start(f32[256]{0:T(256)} %param.17) | copy-start | bytes 3076
  116.2 100.2 %copy-start.132 = (f32[256]{0:T(256)S(1)}, f32[256]{0:T(256)}, u32[]{:S(2)}) copy-start(f32[256]{0:T(256)} %param.15) | copy-start | bytes 3076
  206.9 18.2 %copy-start.12 = (bf16[128,32,256]{2,0,1:T(8,128)(2,1)}, bf16[128,32,256]{2,0,1:T(8,128)(2,1)S(1)}, u32[]{:S(2)}) copy-start(bf16[128,32,256]{2,0,1:T(8,128)(2,1)S(1)} %all-to-all-done.1) | copy-start | bytes 6291460
  206.9 387.0 %all-to-all-start.2 = ((bf16[128,32,256]{2,0,1:T(8,128)(2,1)}), bf16[128,32,256]{2,0,1:T(8,128)(2,1)}, u32[]{:S(2)}, u32[]{:S(2)}) async-start(bf16[128,32,256]{2,0,1:T(8,128)(2,1)} %bitcast.49), calls=%async_computation.2 | async-start | bytes 4194304 | tf_op jit(solution)/shard_map/all_to_all | solution.py:106
  234.5 39.7 %copy-start.19 = (f32[256,256]{1,0:T(8,128)}, f32[256,256]{1,0:T(8,128)S(1)}, u32[]{:S(2)}) copy-start(f32[256,256]{1,0:T(8,128)S(1)} %get-tuple-element.41) | copy-start | bytes 786436
  253.3 20.9 %copy-start.107 = (f32[256,16]{1,0:T(8,128)}, f32[256,16]{1,0:T(8,128)S(1)}, u32[]{:S(2)}) copy-start(f32[256,16]{1,0:T(8,128)S(1)} %get-tuple-element.99) | copy-start | bytes 49156
  253.3 20.9 %copy-start.49 = (f32[256,16]{1,0:T(8,128)}, f32[256,16]{1,0:T(8,128)S(1)}, u32[]{:S(2)}) copy-start(f32[256,16]{1,0:T(8,128)S(1)} %get-tuple-element.100) | copy-start | bytes 49156
  253.3 20.9 %copy-start.51 = (f32[256,16]{1,0:T(8,128)}, f32[256,16]{1,0:T(8,128)S(1)}, u32[]{:S(2)}) copy-start(f32[256,16]{1,0:T(8,128)S(1)} %get-tuple-element.101) | copy-start | bytes 49156
  253.3 20.9 %copy-start.53 = (f32[256,16]{1,0:T(8,128)}, f32[256,16]{1,0:T(8,128)S(1)}, u32[]{:S(2)}) copy-start(f32[256,16]{1,0:T(8,128)S(1)} %get-tuple-element.102) | copy-start | bytes 49156
  368.7 24.2 %copy-start.14 = (f32[64,16,256]{2,1,0:T(8,128)S(1)}, f32[64,16,256]{2,1,0:T(8,128)}, u32[]{:S(2)}) copy-start(f32[64,16,256]{2,1,0:T(8,128)} %add.355) | copy-start | bytes 3145732
  472.1 42.3 %copy-start.105 = (f32[256,16]{1,0:T(8,128)S(1)}, f32[256,16]{1,0:T(8,128)}, u32[]{:S(2)}) copy-start(f32[256,16]{1,0:T(8,128)} %get-tuple-element.107) | copy-start | bytes 49156
  548.8 12.7 %copy-start.45 = (f32[256,16]{1,0:T(8,128)S(1)}, f32[256,16]{1,0:T(8,128)}, u32[]{:S(2)}) copy-start(f32[256,16]{1,0:T(8,128)} %get-tuple-element.98) | copy-start | bytes 49156
  548.8 12.7 %copy-start.47 = (f32[256,16]{1,0:T(8,128)S(1)}, f32[256,16]{1,0:T(8,128)}, u32[]{:S(2)}) copy-start(f32[256,16]{1,0:T(8,128)} %get-tuple-element.104) | copy-start | bytes 49156
  548.8 12.7 %copy-start.48 = (f32[256,16]{1,0:T(8,128)S(1)}, f32[256,16]{1,0:T(8,128)}, u32[]{:S(2)}) copy-start(f32[256,16]{1,0:T(8,128)} %get-tuple-element.105) | copy-start | bytes 49156
  548.8 12.7 %copy-start.50 = (f32[256,16]{1,0:T(8,128)S(1)}, f32[256,16]{1,0:T(8,128)}, u32[]{:S(2)}) copy-start(f32[256,16]{1,0:T(8,128)} %copy-done.49) | copy-start | bytes 49156
  548.8 12.7 %copy-start.57 = (f32[256,256]{1,0:T(8,128)S(1)}, f32[256,256]{1,0:T(8,128)}, u32[]{:S(2)}) copy-start(f32[256,256]{1,0:T(8,128)} %get-tuple-element.42) | copy-start | bytes 786436
  548.8 12.7 %copy-start.58 = (f32[256,256]{1,0:T(8,128)S(1)}, f32[256,256]{1,0:T(8,128)}, u32[]{:S(2)}) copy-start(f32[256,256]{1,0:T(8,128)} %get-tuple-element.46) | copy-start | bytes 786436
  596.8 56.6 %copy-start.1 = (bf16[256,256]{1,0:T(8,128)(2,1)S(1)}, bf16[256,256]{1,0:T(8,128)(2,1)}, u32[]{:S(2)}) copy-start(bf16[256,256]{1,0:T(8,128)(2,1)} %param.16) | copy-start | bytes 393220
  (115 other events, 671.9 us)
Sparse Core Ops, SparseCore 0:
  9.8 87.7 all-gather.2
  102.1 102.2 all-gather.4
where the time goes:
time: 667 us; the launch traced here: 660 us
  local copies, waits for them, and re-layouts  226 us (34%)
  other arithmetic  167 us (25%)
  waiting for transfers between devices  150 us (22%)
  blocking collectives  55.1 us (8%)
  starting transfers between devices  33.6 us (5%)
  between operations  15.2 us (2%)
  matrix products  13.1 us (2%)
    pad x12, local copies, waits for them, and re-layouts, selective_scan(): _, through = lax.associative_scan(link_blocks, (totals, state), axis=0)  99.8 us
    all_gather x1, waiting for transfers between devices, local(): proj = lax.all_gather(local_proj, 'seq', axis=0, tiled=True)  88.2 us
    reduce_sum x8, other arithmetic, selective_scan(): local_parts.append(jnp.sum(c_now[:, :, None] * state, axis=1))  74.5 us
    all_gather x1, waiting for transfers between devices, local(): lax.all_gather(x_weight, 'seq', axis=0, tiled=True)  59.4 us
    all_to_all x1, blocking collectives, local(): return lax.all_to_all(gated, 'seq', split_axis=0, concat_axis=1, tiled=True)  55.1 us
    unnamed x267, local copies, waits for them, and re-layouts  46.1 us
    slice x1, local copies, waits for them, and re-layouts, selective_scan(): through[:blocks - 1]  40.5 us
    reduce_sum x2, other arithmetic, selective_scan(): jnp.sum(c_now[:, :, None] * jnp.exp(elapsed[place][:, None, :] * rate[Non...  17.5 us
  transfers between devices with their start and end apart: 6, of which 3 were waited for; matrix products, arithmetic and copies ran while one was open for 59% of the time, Pallas kernels for 0%

commit v1 on v0

--- a/solution.py
+++ b/solution.py
@@ -2,6 +2,15 @@
 import jax.numpy as jnp
 from jax import lax
 from jax.sharding import PartitionSpec as P
+
+
+def search_the_thing(local_block):
+    parts_n = lax.psum(1, "seq")
+    shaped = tuple((parts_n if ix == 0 else 1 for ix in range(local_block.ndim)))
+    value_now = lax.all_to_all(
+        jnp.tile(local_block, shaped), "seq", tiled=True, concat_axis=0, split_axis=0
+    )
+    return value_now
 
 
 def passed_along(value, axis, steps):
@@ -96,11 +105,7 @@
     prior = passed_along(conv_input[conv_input.shape[0] - (width - 1) :], "seq", 1)
     params = gather_directly(jnp.concatenate([conv_weight, conv_bias[None, :]], 0), "seq", 1)
     outgoing = causal_conv(prior.astype(jnp.float32), conv_input, params[:width], params[width])
-    local_proj = jnp.dot(
-        outgoing,
-        lax.all_gather(x_weight, "seq", axis=0, tiled=True),
-        preferred_element_type=jnp.float32,
-    )
+    local_proj = jnp.dot(outgoing, search_the_thing(x_weight), preferred_element_type=jnp.float32)
     arrived, gate_part = (
         lax.all_to_all(outgoing, "seq", split_axis=1, concat_axis=0, tiled=True),
         lax.all_to_all(gate_input, "seq", split_axis=1, concat_axis=0, tiled=True),

time: 667 us -> 725 us (1.087)
  waiting for transfers between devices: 150 us -> 192 us
  blocking collectives: 55.1 us -> 76 us
  other arithmetic: 167 us -> 159 us
    ppermute x1, waiting for transfers between devices: 0.01 us -> 96.7 us  [passed_along(): lax.ppermute(value, axis, [(source, source + steps) for source in range(i...]
    all_gather x1 -> x0, waiting for transfers between devices: 59.4 us -> none  [local(): lax.all_gather(x_weight, 'seq', axis=0, tiled=True)]
    all_to_all x0 -> x1, blocking collectives: none -> 20.9 us  [from_everyone(): return lax.all_to_all(copies, axis, split_axis=0, concat_axis=0, tiled=True)]
    unnamed x267 -> x269, local copies, waits for them, and re-layouts: 46.1 us -> 46.1 us
  transfers between devices with their start and end apart: 6 -> 5, of which waited for: 3 -> 3; matrix products, arithmetic and copies ran while one was open for 59% -> 53% of each run, Pallas kernels for 0% -> 0%
where the time goes in v1:
time: 725 us; the launch traced here: 713 us
  local copies, waits for them, and re-layouts  232 us (32%)
  waiting for transfers between devices  192 us (26%)
  other arithmetic  159 us (22%)
  blocking collectives  76 us (10%)
  starting transfers between devices  28.4 us (4%)
  between operations  15.5 us (2%)
  matrix products  10.9 us (2%)
    pad x12, local copies, waits for them, and re-layouts, selective_scan(): _, through = lax.associative_scan(link_blocks, (totals, state), axis=0)  99.8 us
    ppermute x1, waiting for transfers between devices, passed_along(): lax.ppermute(value, axis, [(source, source + steps) for source in range(i...  96.7 us
    all_gather x1, waiting for transfers between devices, local(): proj = lax.all_gather(local_proj, 'seq', axis=0, tiled=True)  92.1 us
    reduce_sum x8, other arithmetic, selective_scan(): local_parts.append(jnp.sum(c_now[:, :, None] * state, axis=1))  74.5 us
    all_to_all x1, blocking collectives, local(): return lax.all_to_all(gated, 'seq', split_axis=0, concat_axis=1, tiled=True)  55.1 us
    unnamed x269, local copies, waits for them, and re-layouts  46.1 us
    slice x1, local copies, waits for them, and re-layouts, selective_scan(): through[:blocks - 1]  40.5 us
    all_to_all x1, blocking collectives, from_everyone(): return lax.all_to_all(copies, axis, split_axis=0, concat_axis=0, tiled=True)  20.9 us
  transfers between devices with their start and end apart: 5, of which 3 were waited for; matrix products, arithmetic and copies ran while one was open for 53% of the time, Pallas kernels for 0%

profile of v1, /device:TPU:32, one launch (start us, length us, event | category | flops | bytes accessed | tf_op | source)
XLA Modules:
  0.0 713.1 jit_solution(1274582521403100421)
XLA Ops:
  7.9 20.9 %all_to_all.59 = bf16[32,5,256]{2,1,0:T(8,128)(2,1)S(1)} all-to-all(bf16[32,5,256]{2,1,0:T(8,128)(2,1)S(1)} %broadcast_in_dim.7), channel_id=1, replica_groups=mesh['seq'=32,'batch'=8] {'seq'}, dimensions={0} | all-to-all | bytes 163840 | tf_op jit(solution)/shard_map/all_to_all | solution.py:24
  41.7 96.7 %collective-permute-done = bf16[3,8192]{1,0:T(4,128)(2,1)S(1)} collective-permute-done((bf16[3,8192]{1,0:T(4,128)(2,1)S(1)}, bf16[3,8192]{1,0:T(4,128)(2,1)S(1)}, u32[]{:S(2)}, u32[]{:S(2)}) %collective-permute-start) | collective-permute-done | bytes 49184 | tf_op jit(solution)/shard_map/ppermute | solution.py:19
  151.4 9.6 %all-to-all-start.2 = ((bf16[128,32,256]{2,0,1:T(8,128)(2,1)}), bf16[128,32,256]{2,0,1:T(8,128)(2,1)S(1)}, u32[]{:S(2)}, u32[]{:S(2)}) async-start(bf16[128,32,256]{2,0,1:T(8,128)(2,1)} %bitcast.53), calls=%async_computation.2 | async-start | bytes 4194304 | tf_op jit(solution)/shard_map/all_to_all | solution.py:110
  164.2 92.1 %all-gather.2.cloned.1.call-done = f32[4096,288]{0,1:T(8,128)} async-done(((f32[128,288]{0,1:T(8,128)}), f32[4096,288]{0,1:T(8,128)}) %all-gather.2.cloned.1.call-update) | async-done | bytes 4718608 | tf_op jit(solution)/shard_map/all_gather | solution.py:113
  258.9 10.0 %all-to-all-start.3 = ((bf16[128,32,256]{2,0,1:T(8,128)(2,1)}), bf16[128,32,256]{2,0,1:T(8,128)(2,1)}, u32[]{:S(2)}, u32[]{:S(2)}) async-start(bf16[128,32,256]{2,0,1:T(8,128)(2,1)} %bitcast.52), calls=%async_computation.3 | async-start | bytes 4194304 | tf_op jit(solution)/shard_map/all_to_all | solution.py:111
  268.9 8.7 %bitcast_multiply_fusion.2 = (f32[4096,256]{1,0:T(8,128)}, f32[4096,256]{1,0:T(8,128)}) fusion(bf16[128,32,256]{2,0,1:T(8,128)(2,1)S(1)} %all-to-all-done.2, f32[256]{0:T(256)S(1)} %copy-done.132, bf16[256,256]{1,0:T(8,128)(2,1)S(1)} %copy-done, f32[4096,288]{0,1:T(8,128)} %all-gather.2.cloned.1.call-done, f32[256]{0:T(256)S(1)} %copy-done.133, ...), kind=kOutput, calls=%fused_computation.23 | convolution fusion | flops 549453824 | bytes 14829568 | tf_op jit(solution)/shard_map/dot_general | solution.py:123
  306.7 20.0 %multiply_reduce_fusion.1 = (f32[256,256]{1,0:T(8,128)}, f32[256,16,256]{2,1,0:T(8,128)S(1)}, f32[256,16,256]{2,1,0:T(8,128)S(1)}, f32[256,16,256]{2,1,0:T(8,128)}) fusion(f32[256,16]{1,0:T(8,128)S(1)} %get-tuple-element.99, f32[256,256]{1,0:T(8,128)} %get-tuple-element.77, f32[256,16]{1,0:T(8,128)} %get-tuple-element.117, ...), kind=kLoop, calls=%fused_computation.27 | loop fusion | flops 69140480 | bytes 21528576 | tf_op jit(solution)/shard_map/reduce_sum | solution.py:74
  326.8 6.3 multiply_reduce_fusion.3
  375.8 8.7 %pad.59 = f32[32,16,256]{2,1,0:T(8,128)} pad(f32[16,16,256]{2,1,0:T(8,128)} %add.351, f32[]{:T(128)} %constant.5.clone.1), padding=1_0_1x0_0_0x0_0_0 | pad | bytes 786436 | tf_op jit(solution)/shard_map/pad | solution.py:78
  389.0 11.6 %pad.61 = f32[64,16,256]{2,1,0:T(8,128)S(1)} pad(f32[32,16,256]{2,1,0:T(8,128)} %add.353, f32[]{:T(128)} %constant.5.clone.1), padding=1_0_1x0_0_0x0_0_0 | pad | bytes 1572868 | tf_op jit(solution)/shard_map/pad | solution.py:78
  402.4 15.6 %pad.60 = f32[64,16,256]{2,1,0:T(8,128)} pad(f32[32,16,256]{2,1,0:T(8,128)} %pad_maximum_fusion.3, f32[]{:T(128)} %constant.5.clone.1), padding=0_1_1x0_0_0x0_0_0 | pad | bytes 1572868 | tf_op jit(solution)/shard_map/pad | solution.py:78
  422.4 23.1 %pad.62 = f32[128,16,256]{2,1,0:T(8,128)S(1)} pad(f32[64,16,256]{2,1,0:T(8,128)} %pad_maximum_fusion.2, f32[]{:T(128)} %constant.5.clone.1), padding=0_1_1x0_0_0x0_0_0 | pad | bytes 3145732 | tf_op jit(solution)/shard_map/pad | solution.py:78
  445.6 20.5 %pad.63 = f32[128,16,256]{2,1,0:T(8,128)} pad(f32[64,16,256]{2,1,0:T(8,128)S(1)} %copy-done.14, f32[]{:T(128)} %constant.5.clone.1), padding=1_0_1x0_0_0x0_0_0 | pad | bytes 3145732 | tf_op jit(solution)/shard_map/pad | solution.py:78
  475.1 9.2 %multiply_reduce_fusion.17 = f32[256,256]{1,0:T(8,128)} fusion(f32[256,16]{1,0:T(8,128)S(1)} %copy-done.104, f32[256,256]{1,0:T(8,128)S(1)} %copy-done.94, f32[256,16]{1,0:T(8,128)S(1)} %copy-done.129, f32[256,256]{1,0:T(8,128)S(1)} %copy-done.103, f32[16,256]{1,0:T(8,128)S(1)} %exponential_negate_fusion, f32[256,256]{1,0:T(8,128)S(1)} %copy-done.93, ...), kind=kLoop, calls=%fused_computation.43 | loop fusion | flops 35586048 | bytes 4620288 | tf_op jit(solution)/shard_map/reduce_sum | solution.py:74
  484.3 40.5 %pad.161 = f32[256,16,256]{2,1,0:T(8,128)} pad(f32[128,16,256]{2,1,0:T(8,128)S(1)} %copy-done.11, f32[]{:T(128)} %constant.5.clone.1), padding=1_0_1x0_0_0x0_0_0 | pad | bytes 6291460
  526.6 40.5 %pad.87 = f32[255,16,256]{2,1,0:T(8,128)} pad(f32[128,16,256]{2,1,0:T(8,128)S(1)} %pad_maximum_fusion.1, f32[]{:T(128)} %constant.5.clone.1), padding=0_0_1x0_0_0x0_0_0 | pad | bytes 6275076 | tf_op jit(solution)/shard_map/slice | solution.py:79
  567.2 8.7 %multiply_reduce_fusion.19 = f32[256,256]{1,0:T(8,128)S(1)} fusion(f32[256,16]{1,0:T(8,128)S(1)} %copy-done.106, f32[256,256]{1,0:T(8,128)} %get-tuple-element.86, f32[256,16]{1,0:T(8,128)} %get-tuple-element.126, f32[256,256]{1,0:T(8,128)} %get-tuple-element.87, f32[256,16]{1,0:T(8,128)} %get-tuple-element.127, f32[256,256]{1,0:T(8,128)} %get-tuple-element.65, ...), kind=kLoop, calls=%fused_computation.45 | loop fusion | flops 31391744 | bytes 4079616 | tf_op jit(solution)/shard_map/reduce_sum | solution.py:74
  576.1 6.3 multiply_reduce_fusion.21
  583.9 9.1 %multiply_reduce_fusion.29 = (f32[256,256]{1,0:T(8,128)S(1)}, f32[256,256]{1,0:T(8,128)S(1)}, f32[256,256]{1,0:T(8,128)S(1)}, f32[256,256]{1,0:T(8,128)S(1)}, f32[256,256]{1,0:T(8,128)S(1)}, /*index=5*/f32[256,256]{1,0:T(8,128)S(1)}) fusion(f32[256,16]{1,0:T(8,128)S(1)} %copy-done.114, f32[256,256]{1,0:T(8,128)S(1)} %copy-done.88, ...), kind=kLoop, calls=%fused_computation.55 | loop fusion | flops 27918336 | bytes 7716864 | tf_op jit(solution)/shard_map/reduce_sum | solution.py:74
  593.8 7.5 %multiply_reduce_fusion.23 = (f32[256,256]{1,0:T(8,128)S(1)}, f32[256,256]{1,0:T(8,128)S(1)}, f32[256,256]{1,0:T(8,128)S(1)}) fusion(f32[256,16]{1,0:T(8,128)S(1)} %copy-done.111, f32[256,256]{1,0:T(8,128)S(1)} %copy-done.82, f32[256,16]{1,0:T(8,128)S(1)} %copy-done.118, f32[256,256]{1,0:T(8,128)S(1)} %copy-done.85, f32[256,16]{1,0:T(8,128)S(1)} %copy-done.120, ...), kind=kLoop, calls=%fused_computation.49 | loop fusion | flops 27066368 | bytes 3555328 | tf_op jit(solution)/shard_map/reduce_sum | solution.py:74
  601.6 8.8 %multiply_reduce_fusion = (f32[256,256]{1,0:T(8,128)S(1)}, f32[256,256]{1,0:T(8,128)S(1)}, f32[256,256]{1,0:T(8,128)S(1)}, f32[256,256]{1,0:T(8,128)S(1)}, f32[256,256]{1,0:T(8,128)S(1)}, /*index=5*/f32[256,256]{1,0:T(8,128)S(1)}) fusion(f32[256,16]{1,0:T(8,128)S(1)} %copy-done.109, f32[16,256]{1,0:T(8,128)S(1)} %exponential_negate_fusion, ...), kind=kLoop, calls=%fused_computation.26 | loop fusion | flops 24772608 | bytes 7438336 | tf_op jit(solution)/shard_map/reduce_sum | solution.py:83
  614.5 8.8 %multiply_reduce_fusion.2 = (f32[256,256]{1,0:T(8,128)S(1)}, f32[256,256]{1,0:T(8,128)S(1)}, f32[256,256]{1,0:T(8,128)S(1)}, f32[256,256]{1,0:T(8,128)S(1)}, f32[256,256]{1,0:T(8,128)S(1)}, /*index=5*/f32[256,256]{1,0:T(8,128)S(1)}) fusion(f32[256,256]{1,0:T(8,128)S(1)} %copy-done.58, f32[256,16]{1,0:T(8,128)S(1)} %copy-done.51, ...), kind=kLoop, calls=%fused_computation.28 | loop fusion | flops 24772608 | bytes 7438336 | tf_op jit(solution)/shard_map/reduce_sum | solution.py:83
  624.9 7.2 %multiply_reduce_fusion.9 = (f32[256,256]{1,0:T(8,128)S(1)}, f32[256,256]{1,0:T(8,128)S(1)}, f32[256,256]{1,0:T(8,128)S(1)}, f32[256,256]{1,0:T(8,128)S(1)}) fusion(f32[256,16]{1,0:T(8,128)S(1)} %copy-done.47, f32[256,256]{1,0:T(8,128)S(1)} %copy-done.28, f32[256,16]{1,0:T(8,128)S(1)} %copy-done.41, f32[256,256]{1,0:T(8,128)S(1)} %copy-done.38, ...), kind=kLoop, calls=%fused_computation.35 | loop fusion | flops 20709376 | bytes 6946816 | tf_op jit(solution)/shard_map/reduce_sum | solution.py:74
  649.5 55.1 %all_to_all.60 = bf16[32,128,256]{2,1,0:T(8,128)(2,1)S(1)} all-to-all(bf16[32,128,256]{2,1,0:T(8,128)(2,1)S(1)} %bitcast.51), channel_id=1, replica_groups=mesh['seq'=32,'batch'=8] {'seq'}, dimensions={0} | all-to-all | bytes 4194304 | tf_op jit(solution)/shard_map/all_to_all | solution.py:133
  (366 shorter events, 152.1 us)
Async XLA Ops:
  6.5 262.4 %copy-start = (bf16[256,256]{1,0:T(8,128)(2,1)S(1)}, bf16[256,256]{1,0:T(8,128)(2,1)}, u32[]{:S(2)}) copy-start(bf16[256,256]{1,0:T(8,128)(2,1)} %param.16) | copy-start | bytes 393220
  32.5 112.2 %all-to-all-start.1 = ((bf16[32,256,288]{1,2,0:T(8,128)(2,1)}), bf16[32,256,288]{1,2,0:T(8,128)(2,1)}, u32[]{:S(2)}, u32[]{:S(2)}) async-start(bf16[32,256,288]{1,2,0:T(8,128)(2,1)} %tile.2), calls=%async_computation.1 | async-start | bytes 9437184 | tf_op jit(solution)/shard_map/all_to_all | solution.py:10
  37.8 218.5 %all-gather.2.cloned.1.call-start = ((), (), s32[]{:S(2)}) async-start(), calls=%async_computation.5 | async-start | bytes 4866048 | tf_op jit(solution)/shard_map/all_gather | solution.py:113
  37.9 100.5 %collective-permute-start = (bf16[3,8192]{1,0:T(4,128)(2,1)S(1)}, bf16[3,8192]{1,0:T(4,128)(2,1)S(1)}, u32[]{:S(2)}, u32[]{:S(2)}) collective-permute-start(bf16[3,8192]{1,0:T(4,128)(2,1)S(1)} %slice.443), channel_id=1, source_target_pairs={{0,8},{8,16},{16,24},{24,32},{32,40},{40,48},{48,56},{56,64},{64,7... | collective-permute-start | bytes 147464 | tf_op jit(solution)/shard_map/ppermute | solution.py:19
  151.4 107.4 %all-to-all-start.2 = ((bf16[128,32,256]{2,0,1:T(8,128)(2,1)}), bf16[128,32,256]{2,0,1:T(8,128)(2,1)S(1)}, u32[]{:S(2)}, u32[]{:S(2)}) async-start(bf16[128,32,256]{2,0,1:T(8,128)(2,1)} %bitcast.53), calls=%async_computation.2 | async-start | bytes 4194304 | tf_op jit(solution)/shard_map/all_to_all | solution.py:110
  164.2 104.7 %copy-start.132 = (f32[256]{0:T(256)S(1)}, f32[256]{0:T(256)}, u32[]{:S(2)}) copy-start(f32[256]{0:T(256)} %param.17) | copy-start | bytes 3076
  164.2 104.7 %copy-start.133 = (f32[256]{0:T(256)S(1)}, f32[256]{0:T(256)}, u32[]{:S(2)}) copy-start(f32[256]{0:T(256)} %param.15) | copy-start | bytes 3076
  258.8 18.8 %copy-start.12 = (bf16[128,32,256]{2,0,1:T(8,128)(2,1)}, bf16[128,32,256]{2,0,1:T(8,128)(2,1)S(1)}, u32[]{:S(2)}) copy-start(bf16[128,32,256]{2,0,1:T(8,128)(2,1)S(1)} %all-to-all-done.2) | copy-start | bytes 6291460
  258.9 387.7 %all-to-all-start.3 = ((bf16[128,32,256]{2,0,1:T(8,128)(2,1)}), bf16[128,32,256]{2,0,1:T(8,128)(2,1)}, u32[]{:S(2)}, u32[]{:S(2)}) async-start(bf16[128,32,256]{2,0,1:T(8,128)(2,1)} %bitcast.52), calls=%async_computation.3 | async-start | bytes 4194304 | tf_op jit(solution)/shard_map/all_to_all | solution.py:111
  287.1 39.7 %copy-start.20 = (f32[256,256]{1,0:T(8,128)}, f32[256,256]{1,0:T(8,128)S(1)}, u32[]{:S(2)}) copy-start(f32[256,256]{1,0:T(8,128)S(1)} %get-tuple-element.41) | copy-start | bytes 786436
  305.9 20.9 %copy-start.108 = (f32[256,16]{1,0:T(8,128)}, f32[256,16]{1,0:T(8,128)S(1)}, u32[]{:S(2)}) copy-start(f32[256,16]{1,0:T(8,128)S(1)} %get-tuple-element.99) | copy-start | bytes 49156
  305.9 20.9 %copy-start.50 = (f32[256,16]{1,0:T(8,128)}, f32[256,16]{1,0:T(8,128)S(1)}, u32[]{:S(2)}) copy-start(f32[256,16]{1,0:T(8,128)S(1)} %get-tuple-element.100) | copy-start | bytes 49156
  305.9 20.9 %copy-start.52 = (f32[256,16]{1,0:T(8,128)}, f32[256,16]{1,0:T(8,128)S(1)}, u32[]{:S(2)}) copy-start(f32[256,16]{1,0:T(8,128)S(1)} %get-tuple-element.101) | copy-start | bytes 49156
  305.9 20.9 %copy-start.54 = (f32[256,16]{1,0:T(8,128)}, f32[256,16]{1,0:T(8,128)S(1)}, u32[]{:S(2)}) copy-start(f32[256,16]{1,0:T(8,128)S(1)} %get-tuple-element.102) | copy-start | bytes 49156
  421.3 24.2 %copy-start.14 = (f32[64,16,256]{2,1,0:T(8,128)S(1)}, f32[64,16,256]{2,1,0:T(8,128)}, u32[]{:S(2)}) copy-start(f32[64,16,256]{2,1,0:T(8,128)} %add.355) | copy-start | bytes 3145732
  524.8 42.3 %copy-start.106 = (f32[256,16]{1,0:T(8,128)S(1)}, f32[256,16]{1,0:T(8,128)}, u32[]{:S(2)}) copy-start(f32[256,16]{1,0:T(8,128)} %get-tuple-element.107) | copy-start | bytes 49156
  601.4 12.8 %copy-start.46 = (f32[256,16]{1,0:T(8,128)S(1)}, f32[256,16]{1,0:T(8,128)}, u32[]{:S(2)}) copy-start(f32[256,16]{1,0:T(8,128)} %get-tuple-element.98) | copy-start | bytes 49156
  601.4 12.8 %copy-start.48 = (f32[256,16]{1,0:T(8,128)S(1)}, f32[256,16]{1,0:T(8,128)}, u32[]{:S(2)}) copy-start(f32[256,16]{1,0:T(8,128)} %get-tuple-element.104) | copy-start | bytes 49156
  601.5 12.8 %copy-start.49 = (f32[256,16]{1,0:T(8,128)S(1)}, f32[256,16]{1,0:T(8,128)}, u32[]{:S(2)}) copy-start(f32[256,16]{1,0:T(8,128)} %get-tuple-element.105) | copy-start | bytes 49156
  601.5 12.8 %copy-start.51 = (f32[256,16]{1,0:T(8,128)S(1)}, f32[256,16]{1,0:T(8,128)}, u32[]{:S(2)}) copy-start(f32[256,16]{1,0:T(8,128)} %copy-done.50) | copy-start | bytes 49156
  601.5 12.8 %copy-start.58 = (f32[256,256]{1,0:T(8,128)S(1)}, f32[256,256]{1,0:T(8,128)}, u32[]{:S(2)}) copy-start(f32[256,256]{1,0:T(8,128)} %get-tuple-element.42) | copy-start | bytes 786436
  601.5 12.8 %copy-start.59 = (f32[256,256]{1,0:T(8,128)S(1)}, f32[256,256]{1,0:T(8,128)}, u32[]{:S(2)}) copy-start(f32[256,256]{1,0:T(8,128)} %get-tuple-element.46) | copy-start | bytes 786436
  601.5 12.8 %copy-start.60 = (f32[256,256]{1,0:T(8,128)S(1)}, f32[256,256]{1,0:T(8,128)}, u32[]{:S(2)}) copy-start(f32[256,256]{1,0:T(8,128)} %get-tuple-element.47) | copy-start | bytes 786436
  649.4 56.6 %copy-start.1 = (bf16[256,256]{1,0:T(8,128)(2,1)S(1)}, bf16[256,256]{1,0:T(8,128)(2,1)}, u32[]{:S(2)}) copy-start(bf16[256,256]{1,0:T(8,128)(2,1)} %param.16) | copy-start | bytes 393220
  (115 other events, 665.2 us)
Sparse Core Ops, SparseCore 0:
  149.9 106.2 all-gather.1
